TPU v7x, 32 devices: a whole 2x2x4 slice. The times are simulated.
32 devices in a mesh: blk: 4 (over z), tp: 8 (over y, x, core).
Axes of the slice: x: 2, y: 2, z: 4, core: 2. Of those that a mesh axis runs over, the one named last changes fastest.
Arguments:
- input_pool: bfloat16 [4096, 1792], P(None, 'tp'), may hold values from -6 to 6
- teacher_pool: bfloat16 [4096, 1792], P(None, 'tp'), may hold values from -6 to 6
- gate_weight: bfloat16 [1792, 9472], P(None, 'tp'), may hold values from -0.125 to 0.125
- up_weight: bfloat16 [1792, 9472], P(None, 'tp'), may hold values from -0.125 to 0.125
- params: float32 [4, 9472, 1792], P('blk', 'tp'), may hold values from -6 to 6
- batch_ids: int32 [4, 1024], replicated, may hold values from 0 to 4095
- cycle_order: int32 [4], replicated, may hold values from 0 to 3, each once
- edge_weight: float32 [4], replicated, may hold values from 0.1 to 0.45
Outputs:
- updated: float32 [4, 9472, 1792], P('blk', 'tp')
Inputs may be any that keep to these rules, and one draw needn't show every extreme that they name: `cycle_order`: the 4 cycle positions name 4 different agents.
All inputs are finite; a program needn't handle non-finite values.
Results may differ from a plain program's by a relative error of at most 0.0061.
Values may be sent and summed in bfloat16 or wider, within the bound.
A program may use at most 128 MiB of HBM per device.

v0:
```python
import jax
import jax.numpy as jnp
from jax import lax
from jax.sharding import PartitionSpec as P


def shifted(array, axis, by):
    count = lax.axis_size(axis)
    return lax.ppermute(array, axis, [(i, (i + by) % count) for i in range(count)])


def body(
    input_pool, teacher_pool, gate_weight, up_weight, params, batch_ids, cycle_order, edge_weight
):
    step_rate = 2.0
    groups = lax.axis_size("tp")
    place = lax.axis_index("blk")
    agents = cycle_order.shape[0]
    slots = jnp.arange(agents, dtype=jnp.int32)
    here = slots == place
    before = slots == (place + agents - 1) % agents
    agent = jnp.sum(jnp.where(here, cycle_order, 0))
    weight_next = jnp.sum(jnp.where(here, edge_weight, 0.0))
    weight_prev = jnp.sum(jnp.where(before, edge_weight, 0.0))
    weight_self = 1.0 - weight_next - weight_prev
    batch = lax.dynamic_slice_in_dim(batch_ids, agent, 1, 0)[0]
    inputs_local = jnp.take(input_pool, batch, axis=0)
    teacher_local = jnp.take(teacher_pool, batch, axis=0)
    hidden_dev = gate_weight.shape[1]
    scale = float(hidden_dev * groups) ** (-0.5)
    rows = lax.all_gather(inputs_local, "tp", axis=1, tiled=True)
    gate = jnp.dot(rows, gate_weight, preferred_element_type=jnp.float32)
    up = jnp.dot(rows, up_weight, preferred_element_type=jnp.float32)
    teacher = lax.all_gather(teacher_local, "tp", axis=1, tiled=True)
    gate, up, teacher_full = (gate, up, teacher)
    hidden = (jax.nn.silu(gate) * up).astype(jnp.bfloat16)

    def gradient(weights):
        weights_half = weights.astype(jnp.bfloat16)
        partial_out = scale * jnp.dot(hidden, weights_half, preferred_element_type=jnp.float32)
        output = lax.psum(partial_out, "tp")
        resid = (output - teacher_full.astype(jnp.float32)).astype(jnp.bfloat16)
        return scale * lax.dot_general(
            hidden, resid, (((0,), (0,)), ((), ())), preferred_element_type=jnp.float32
        )

    start_field = params[0]
    grad_first = gradient(start_field)

    def mix_two(field):
        lower = shifted(field, "blk", 1)
        upper = shifted(field, "blk", -1)
        return weight_self * field + weight_next * upper + weight_prev * lower

    moved = mix_two(start_field) - step_rate * grad_first
    combined = moved - step_rate * grad_first
    grad_second = gradient(moved)
    result = mix_two(combined) - step_rate * (grad_second - grad_first)
    return result[None]


def solution(mesh):
    placed = (
        P(None, "tp"),
        P(None, "tp"),
        P(None, "tp"),
        P(None, "tp"),
        P("blk", "tp", None),
        P(),
        P(),
        P(),
    )
    return jax.shard_map(
        body, mesh=mesh, in_specs=placed, out_specs=P("blk", "tp", None), check_vma=False
    )
```

profile of v0, /device:TPU:0, one launch (start us, length us, event | category | flops | bytes accessed | tf_op | source)
XLA Modules:
  0.0 809.0 jit_solution(17603481513020024617)
XLA Ops:
  6.5 0.0 copy-start
  6.5 0.0 all-gather.3.cloned.1.call-start
  6.5 1.3 fusion.11
  9.8 0.0 copy-done
  9.8 4.0 copy.11
  13.8 3.2 copy.13
  17.0 5.3 gather_fusion
  22.4 3.9 gather_fusion.1
  26.3 0.2 broadcast_select_fusion
  26.5 1.0 copy.12
  27.5 0.0 all-gather.3.cloned.1.call-update
  27.5 0.0 all-gather.5.cloned.1.call-start
  27.6 1.0 copy.14
  28.5 0.0 all-gather.5.cloned.1.call-update
  28.5 0.0 all-reduce.3.cloned.1.call-start
  28.6 5.1 collective-permute-start
  33.7 0.0 collective-permute-start.1
  33.7 31.0 %all-gather.3.cloned.1.call-done = bf16[1024,1792]{0,1:T(8,128)(2,1)} async-done(((bf16[1024,224]{0,1:T(8,128)(2,1)}), bf16[1024,1792]{0,1:T(8,128)(2,1)}) %all-gather.3.cloned.1.call-update) | async-done | bytes 3670032 | tf_op jit(solution)/shard_map/all_gather | solution.py:31
  64.8 0.0 copy-start.5
  64.8 0.0 slice-start.3
  64.8 0.0 slice-start.4
  64.8 7.6 fusion.17
  72.3 0.0 copy-done.5
  72.4 0.0 slice-start.5
  72.4 8.0 multiply_convert_fusion
  80.4 0.0 copy-start.2
  80.4 1.5 copy-done.2
  81.8 0.0 slice-done.3
  81.8 0.0 slice-done.4
  81.8 0.0 slice-done.5
  81.8 7.2 convolution_multiply_fusion.2
  89.1 0.0 copy-start.4
  89.1 0.0 all-reduce.3.cloned.1.call-update
  89.1 0.0 all-reduce.5.cloned.1.call-start
  89.1 0.6 copy-done.4
  89.7 0.7 fusion.10
  91.6 9.5 %all-gather.5.cloned.1.call-done = bf16[1024,1792]{0,1:T(8,128)(2,1)} async-done(((bf16[1024,224]{0,1:T(8,128)(2,1)}), bf16[1024,1792]{0,1:T(8,128)(2,1)}) %all-gather.5.cloned.1.call-update) | async-done | bytes 3670032 | tf_op jit(solution)/shard_map/all_gather | solution.py:34
  101.1 115.9 %collective-permute-done = f32[1184,1792]{1,0:T(8,128)} collective-permute-done((f32[1184,1792]{1,0:T(8,128)}, f32[1184,1792]{1,0:T(8,128)}, u32[]{:S(2)}, u32[]{:S(2)}) %collective-permute-start) | collective-permute-done | bytes 8486944 | tf_op jit(solution)/shard_map/ppermute | solution.py:9
  217.0 181.6 %collective-permute-done.1 = f32[1184,1792]{1,0:T(8,128)} collective-permute-done((f32[1184,1792]{1,0:T(8,128)}, f32[1184,1792]{1,0:T(8,128)}, u32[]{:S(2)}, u32[]{:S(2)}) %collective-permute-start.1) | collective-permute-done | bytes 8486944 | tf_op jit(solution)/shard_map/ppermute | solution.py:9
  398.6 0.0 all-reduce.3.cloned.1.call-done
  398.6 22.6 %multiply_subtract_fusion = (f32[1184,1792]{1,0:T(8,128)}, bf16[1184,1792]{1,0:T(8,128)(2,1)S(1)}, f32[1184,1792]{1,0:T(8,128)}) fusion(f32[1184,1792]{1,0:T(8,128)} %collective-permute-done.1, f32[]{:T(128)} %get-tuple-element.7, f32[1184,1792]{1,0:T(8,128)} %collective-permute-done, f32[]{:T(128)} %get-tuple-element.6, f32[1,1184,1792]{2,1,0:T(8,128)} %param.14, ...), kind=kOutput, calls=%fused_computation.9 | convolution fusion | flops 4369899520 | bytes 60112908 | tf_op jit(solution)/shard_map/dot_general | solution.py:43
  421.2 1.6 collective-permute-start.3
  422.9 2.2 collective-permute-start.2
  425.1 8.7 %convolution_multiply_fusion.1 = f32[1024,1792]{0,1:T(8,128)} fusion(bf16[1024,1184]{0,1:T(8,128)(2,1)} %copy-done.2, bf16[1184,1792]{1,0:T(8,128)(2,1)S(1)} %get-tuple-element.9), kind=kOutput, calls=%fused_computation.13 | convolution fusion | flops 4347133952 | bytes 14008320 | tf_op jit(solution)/shard_map/dot_general | solution.py:40
  433.8 0.0 copy-start.3
  433.8 0.0 slice-start
  433.8 0.0 all-reduce.5.cloned.1.call-update
  433.8 113.8 %all-reduce.5.cloned.1.call-done = f32[1024,1792]{0,1:T(8,128)} async-done(((f32[1024,1792]{0,1:T(8,128)}), f32[1024,1792]{0,1:T(8,128)}) %all-reduce.5.cloned.1.call-update) | async-done | bytes 7340048 | tf_op jit(solution)/shard_map/psum | solution.py:41
  547.6 0.0 copy-done.3
  547.6 0.0 slice-start.1
  547.6 0.0 slice-start.2
  547.6 12.8 %fusion.1 = f32[1184,1792]{1,0:T(8,128)} fusion(bf16[1024,1184]{0,1:T(8,128)(2,1)S(1)} %copy-done.3, f32[1184,1792]{1,0:T(8,128)} %get-tuple-element.12, f32[1024,1792]{0,1:T(8,128)} %all-reduce.5.cloned.1.call-done, bf16[1024,1792]{0,1:T(8,128)(2,1)} %all-gather.5.cloned.1.call-done), kind=kOutput, calls=%fused_computation.6 | convolution fusion | flops 4359290880 | bytes 30408704 | tf_op jit(solution)/shard_map/dot_general | solution.py:43
  560.5 48.3 %collective-permute-done.3 = f32[1184,1792]{1,0:T(8,128)} collective-permute-done((f32[1184,1792]{1,0:T(8,128)}, f32[1184,1792]{1,0:T(8,128)}, u32[]{:S(2)}, u32[]{:S(2)}) %collective-permute-start.3) | collective-permute-done | bytes 8486944 | tf_op jit(solution)/shard_map/ppermute | solution.py:9
  608.8 179.5 %collective-permute-done.2 = f32[1184,1792]{1,0:T(8,128)} collective-permute-done((f32[1184,1792]{1,0:T(8,128)}, f32[1184,1792]{1,0:T(8,128)}, u32[]{:S(2)}, u32[]{:S(2)}) %collective-permute-start.2) | collective-permute-done | bytes 8486944 | tf_op jit(solution)/shard_map/ppermute | solution.py:9
  788.3 0.0 slice-done
  788.3 0.0 slice-done.1
  788.3 0.0 slice-done.2
  788.3 0.0 copy-start.1
  788.3 14.1 %subtract_bitcast_fusion = f32[1,1184,1792]{2,1,0:T(8,128)} fusion(f32[1184,1792]{1,0:T(8,128)} %fusion.1, f32[1184,1792]{1,0:T(8,128)} %collective-permute-done.3, f32[1184,1792]{1,0:T(8,128)} %collective-permute-done.2, f32[1184,1792]{1,0:T(8,128)S(1)} %bitcast.29, f32[]{:T(128)} %get-tuple-element.7, f32[]{:T(128)} %get-tuple-element.6, f32[]{:T(128)S(6)} %sub.29), kind=kLoop, calls=%fused_computation.7 | loop fusion | flops 12730368 | bytes 42434572 | tf_op jit(solution)/shard_map/broadcast_in_dim | solution.py:59
  802.4 0.0 copy-done.1
  (5 shorter events, 0.0 us)
Async XLA Ops:
  6.5 3.3 copy-start
  6.5 58.2 %all-gather.3.cloned.1.call-start = ((), (), s32[]{:S(2)}) async-start(), calls=%async_computation | async-start | bytes 4128768 | tf_op jit(solution)/shard_map/all_gather | solution.py:31
  27.5 73.6 %all-gather.5.cloned.1.call-start = ((), (), s32[]{:S(2)}) async-start(), calls=%async_computation.2 | async-start | bytes 4128768 | tf_op jit(solution)/shard_map/all_gather | solution.py:34
  28.5 370.1 %all-reduce.3.cloned.1.call-start = ((), (), s32[]{:S(2)}) async-start(), calls=%async_computation.1 | async-start | bytes 14680064 | tf_op jit(solution)/shard_map/psum | solution.py:41
  28.6 188.4 %collective-permute-start = (f32[1184,1792]{1,0:T(8,128)}, f32[1184,1792]{1,0:T(8,128)}, u32[]{:S(2)}, u32[]{:S(2)}) collective-permute-start(f32[1184,1792]{1,0:T(8,128)} %bitcast.30), channel_id=1, source_target_pairs={{0,24},{8,0},{16,8},{24,16},{1,25},{9,1},{17,9},{25,17},{2,26},{10... | collective-permute-start | bytes 25460744 | tf_op jit(solution)/shard_map/ppermute | solution.py:9
  33.7 364.9 %collective-permute-start.1 = (f32[1184,1792]{1,0:T(8,128)}, f32[1184,1792]{1,0:T(8,128)}, u32[]{:S(2)}, u32[]{:S(2)}) collective-permute-start(f32[1184,1792]{1,0:T(8,128)} %bitcast.31), channel_id=1, source_target_pairs={{0,8},{8,16},{16,24},{24,0},{1,9},{9,17},{17,25},{25,1},{2,10},{10... | collective-permute-start | bytes 25460744 | tf_op jit(solution)/shard_map/ppermute | solution.py:9
  64.8 7.6 copy-start.5
  64.8 17.1 %slice-start.3 = ((s8[8486912]{0:T(1024)(128)(4,1)}), s8[4194304]{0:T(1024)(128)(4,1)S(1)}, s32[]{:S(2)}) async-start(s8[8486912]{0:T(1024)(128)(4,1)} %bitcast.32), calls=%async_computation.7 | async-start | bytes 8388608
  64.8 17.1 %slice-start.4 = ((s8[8486912]{0:T(1024)(128)(4,1)}), s8[4194304]{0:T(1024)(128)(4,1)S(1)}, s32[]{:S(2)}) async-start(s8[8486912]{0:T(1024)(128)(4,1)} %bitcast.32), calls=%async_computation.8 | async-start | bytes 8388608
  72.4 9.5 %slice-start.5 = ((s8[8486912]{0:T(1024)(128)(4,1)}), s8[98304]{0:T(1024)(128)(4,1)S(1)}, s32[]{:S(2)}) async-start(s8[8486912]{0:T(1024)(128)(4,1)} %bitcast.32), calls=%async_computation.9 | async-start | bytes 196608
  80.4 1.5 copy-start.2
  89.1 0.7 copy-start.4
  89.1 458.6 %all-reduce.5.cloned.1.call-start = ((), (), s32[]{:S(2)}) async-start(), calls=%async_computation.3 | async-start | bytes 14680064 | tf_op jit(solution)/shard_map/psum | solution.py:41
  421.2 187.5 %collective-permute-start.3 = (f32[1184,1792]{1,0:T(8,128)}, f32[1184,1792]{1,0:T(8,128)}, u32[]{:S(2)}, u32[]{:S(2)}) collective-permute-start(f32[1184,1792]{1,0:T(8,128)} %get-tuple-element.8), channel_id=1, source_target_pairs={{0,8},{8,16},{16,24},{24,0},{1,9},{9,17},{17,25},{25,1},{2,10},{10... | collective-permute-start | bytes 25460744 | tf_op jit(solution)/shard_map/ppermute | solution.py:9
  422.9 365.4 %collective-permute-start.2 = (f32[1184,1792]{1,0:T(8,128)}, f32[1184,1792]{1,0:T(8,128)}, u32[]{:S(2)}, u32[]{:S(2)}) collective-permute-start(f32[1184,1792]{1,0:T(8,128)} %get-tuple-element.8), channel_id=1, source_target_pairs={{0,24},{8,0},{16,8},{24,16},{1,25},{9,1},{17,9},{25,17},{2,26},{10... | collective-permute-start | bytes 25460744 | tf_op jit(solution)/shard_map/ppermute | solution.py:9
  433.8 113.8 %copy-start.3 = (bf16[1024,1184]{0,1:T(8,128)(2,1)S(1)}, bf16[1024,1184]{0,1:T(8,128)(2,1)}, u32[]{:S(2)}) copy-start(bf16[1024,1184]{0,1:T(8,128)(2,1)} %copy-done.2) | copy-start | bytes 7274500
  433.8 354.5 %slice-start = ((s8[8486912]{0:T(1024)(128)(4,1)}), s8[98304]{0:T(1024)(128)(4,1)S(1)}, s32[]{:S(2)}) async-start(s8[8486912]{0:T(1024)(128)(4,1)} %bitcast.28), calls=%async_computation.4 | async-start | bytes 196608
  547.6 240.6 %slice-start.1 = ((s8[8486912]{0:T(1024)(128)(4,1)}), s8[4194304]{0:T(1024)(128)(4,1)S(1)}, s32[]{:S(2)}) async-start(s8[8486912]{0:T(1024)(128)(4,1)} %bitcast.28), calls=%async_computation.5 | async-start | bytes 8388608
  547.6 240.6 %slice-start.2 = ((s8[8486912]{0:T(1024)(128)(4,1)}), s8[4194304]{0:T(1024)(128)(4,1)S(1)}, s32[]{:S(2)}) async-start(s8[8486912]{0:T(1024)(128)(4,1)} %bitcast.28), calls=%async_computation.6 | async-start | bytes 8388608
  788.3 14.2 %copy-start.1 = (s32[4,1024]{1,0:T(4,128)S(1)}, s32[4,1024]{1,0:T(4,128)}, u32[]{:S(2)}) copy-start(s32[4,1024]{1,0:T(4,128)} %param.15) | copy-start | bytes 49156
Sparse Core Ops, SparseCore 0:
  27.6 37.0 all-gather.2
  66.7 34.3 all-gather.4
  104.4 115.4 all-reduce.2
  433.9 113.6 all-reduce.4
where the time goes:
time: 809 us
  waiting for transfers between devices  680 us (84%)
  matrix products  66.9 us (8%)
  local copies, waits for them, and re-layouts  20.5 us (3%)
  between operations  16.4 us (2%)
  other arithmetic  16.3 us (2%)
  starting transfers between devices  9.08 us (1%)
    ppermute x4, waiting for transfers between devices, shifted(): lax.ppermute(array, axis, [(i, (i + by) % count) for i in range(count)])  525 us
    psum x2, waiting for transfers between devices, gradient(): output = lax.psum(partial_out, 'tp')  114 us
    dot_general x2, matrix products, gradient(): lax.dot_general(hidden, resid, (((0,), (0,)), ((), ())), preferred_elemen...  35.4 us
    all_gather x1, waiting for transfers between devices, body(): rows = lax.all_gather(inputs_local, 'tp', axis=1, tiled=True)  31 us
  transfers between devices with their start and end apart: 8, of which 7 were waited for; matrix products, arithmetic and copies ran while one was open for 6% of the time, Pallas kernels for 0%

commit v1 on v0

--- a/solution.py
+++ b/solution.py
@@ -38,7 +38,7 @@
     def gradient(weights):
         weights_half = weights.astype(jnp.bfloat16)
         partial_out = scale * jnp.dot(hidden, weights_half, preferred_element_type=jnp.float32)
-        output = lax.psum(partial_out, "tp")
+        output = jnp.sum(lax.all_gather(partial_out, "tp"), axis=0)
         resid = (output - teacher_full.astype(jnp.float32)).astype(jnp.bfloat16)
         return scale * lax.dot_general(
             hidden, resid, (((0,), (0,)), ((), ())), preferred_element_type=jnp.float32

time: 809 us -> 875 us (1.082)
  other arithmetic: 16.3 us -> 60.4 us
  waiting for transfers between devices: 680 us -> 703 us
    all_gather x0 -> x2, waiting for transfers between devices: none -> 525 us  [gradient(): output = jnp.sum(lax.all_gather(partial_out, 'tp'), axis=0)]
    ppermute x4, waiting for transfers between devices: 525 us -> 133 us  [shifted(): lax.ppermute(array, axis, [(i, (i + by) % count) for i in range(count)])]
    psum x2 -> x0, waiting for transfers between devices: 114 us -> none  [gradient(): output = lax.psum(partial_out, 'tp')]
    reduce_sum x0 -> x2, other arithmetic: none -> 44 us  [gradient(): output = jnp.sum(lax.all_gather(partial_out, 'tp'), axis=0)]
  transfers between devices with their start and end apart: 8 -> 8, of which waited for: 7 -> 6; matrix products, arithmetic and copies ran while one was open for 6% -> 10% of each run, Pallas kernels for 0% -> 0%
where the time goes in v1:
time: 875 us; the launch traced here: 874 us
  waiting for transfers between devices  703 us (80%)
  matrix products  63 us (7%)
  other arithmetic  60.4 us (7%)
  local copies, waits for them, and re-layouts  24.3 us (3%)
  between operations  16.5 us (2%)
    all_gather x2, waiting for transfers between devices, gradient(): output = jnp.sum(lax.all_gather(partial_out, 'tp'), axis=0)  525 us
    ppermute x4, waiting for transfers between devices, shifted(): lax.ppermute(array, axis, [(i, (i + by) % count) for i in range(count)])  133 us
    reduce_sum x2, other arithmetic, gradient(): output = jnp.sum(lax.all_gather(partial_out, 'tp'), axis=0)  44 us
    all_gather x1, waiting for transfers between devices, body(): rows = lax.all_gather(inputs_local, 'tp', axis=1, tiled=True)  36.2 us
    dot_general x2, matrix products, gradient(): lax.dot_general(hidden, resid, (((0,), (0,)), ((), ())), preferred_elemen...  30.9 us
  transfers between devices with their start and end apart: 8, of which 6 were waited for; matrix products, arithmetic and copies ran while one was open for 10% of the time, Pallas kernels for 0%

profile of v1, /device:TPU:0, one launch (start us, length us, event | category | flops | bytes accessed | tf_op | source)
XLA Modules:
  0.0 874.3 jit_solution(18031532245252376757)
XLA Ops:
  6.5 0.0 copy-start
  6.5 0.0 all-gather.7.cloned.1.call-start
  6.5 1.3 fusion.11
  9.8 0.0 copy-done
  9.8 4.0 copy.15
  13.8 3.2 copy.17
  17.0 5.3 gather_fusion
  22.4 3.9 gather_fusion.1
  26.3 0.2 broadcast_select_fusion
  26.5 1.0 copy.16
  27.5 0.0 all-gather.7.cloned.1.call-update
  27.5 0.0 all-gather.9.cloned.1.call-start
  27.6 1.0 copy.18
  28.5 0.0 all-gather.9.cloned.1.call-update
  28.6 0.0 all-gather.11.cloned.1.call-start
  28.6 36.2 %all-gather.7.cloned.1.call-done = bf16[1024,1792]{0,1:T(8,128)(2,1)} async-done(((bf16[1024,224]{0,1:T(8,128)(2,1)}), bf16[1024,1792]{0,1:T(8,128)(2,1)}) %all-gather.7.cloned.1.call-update) | async-done | bytes 3670032 | tf_op jit(solution)/shard_map/all_gather | solution.py:31
  64.8 0.0 copy-start.3
  64.8 0.0 slice-start
  64.8 0.0 slice-start.1
  64.8 7.6 fusion.17
  72.3 0.0 copy-done.3
  72.4 0.0 slice-start.2
  72.4 8.0 multiply_convert_fusion
  80.4 0.0 slice-done
  80.4 0.0 slice-done.1
  80.4 0.0 slice-done.2
  80.4 7.3 convolution_multiply_fusion.2
  87.7 0.0 copy-start.2
  87.7 0.0 all-gather.11.cloned.1.call-update
  87.7 0.0 all-gather.13.cloned.1.call-start
  87.8 3.4 collective-permute-start
  91.1 0.0 collective-permute-start.1
  91.1 0.0 copy-done.2
  91.1 0.7 fusion.10
  93.1 7.9 all-gather.9.cloned.1.call-done
  101.1 5.9 copy.19
  107.0 263.3 %all-gather.11.cloned.1.call-done = f32[8192,1792]{1,0:T(8,128)} async-done(((f32[1024,1792]{1,0:T(8,128)}), f32[8192,1792]{1,0:T(8,128)}) %all-gather.11.cloned.1.call-update) | async-done | bytes 58720272 | tf_op jit(solution)/shard_map/all_gather | solution.py:41
  370.3 22.0 %reduce_sum.48 = f32[1024,1792]{1,0:T(8,128)} reduce(f32[8,1024,1792]{2,1,0:T(8,128)} %bitcast.30, f32[]{:T(128)} %constant.38.clone.1), dimensions={0}, to_apply=%region_3.5 | reduce | flops 12845056 | bytes 66060292 | tf_op jit(solution)/shard_map/reduce_sum | solution.py:41
  392.2 0.0 collective-permute-done
  392.3 64.3 %collective-permute-done.1 = f32[1184,1792]{1,0:T(8,128)} collective-permute-done((f32[1184,1792]{1,0:T(8,128)}, f32[1184,1792]{1,0:T(8,128)}, u32[]{:S(2)}, u32[]{:S(2)}) %collective-permute-start.1) | collective-permute-done | bytes 8486944 | tf_op jit(solution)/shard_map/ppermute | solution.py:9
  456.6 20.4 %multiply_subtract_fusion = (f32[1184,1792]{1,0:T(8,128)}, bf16[1184,1792]{1,0:T(8,128)(2,1)}, f32[1184,1792]{1,0:T(8,128)}) fusion(f32[1184,1792]{1,0:T(8,128)} %collective-permute-done.1, f32[]{:T(128)} %get-tuple-element.7, f32[1184,1792]{1,0:T(8,128)} %collective-permute-done, f32[]{:T(128)} %get-tuple-element.6, f32[1,1184,1792]{2,1,0:T(8,128)} %param.14, ...), kind=kOutput, calls=%fused_computation.9 | convolution fusion | flops 4369899520 | bytes 60112908 | tf_op jit(solution)/shard_map/dot_general | solution.py:43
  476.9 9.2 %convolution_multiply_fusion.1 = f32[1024,1792]{1,0:T(8,128)} fusion(bf16[1024,1184]{0,1:T(8,128)(2,1)S(1)} %multiply_convert_fusion, bf16[1184,1792]{1,0:T(8,128)(2,1)} %get-tuple-element.9), kind=kOutput, calls=%fused_computation.13 | convolution fusion | flops 4347133952 | bytes 14008320 | tf_op jit(solution)/shard_map/dot_general | solution.py:40
  486.1 0.0 all-gather.13.cloned.1.call-update
  486.2 1.6 collective-permute-start.3
  487.7 2.3 collective-permute-start.2
  490.0 261.9 %all-gather.13.cloned.1.call-done = f32[8192,1792]{1,0:T(8,128)} async-done(((f32[1024,1792]{1,0:T(8,128)}), f32[8192,1792]{1,0:T(8,128)}) %all-gather.13.cloned.1.call-update) | async-done | bytes 58720272 | tf_op jit(solution)/shard_map/all_gather | solution.py:41
  752.0 22.0 %reduce_sum.49 = f32[1024,1792]{1,0:T(8,128)} reduce(f32[8,1024,1792]{2,1,0:T(8,128)} %bitcast.31, f32[]{:T(128)} %constant.38.clone.1), dimensions={0}, to_apply=%region_4.6 | reduce | flops 12845056 | bytes 66060292 | tf_op jit(solution)/shard_map/reduce_sum | solution.py:41
  774.0 10.6 %fusion.1 = f32[1184,1792]{1,0:T(8,128)S(1)} fusion(bf16[1024,1184]{0,1:T(8,128)(2,1)S(1)} %multiply_convert_fusion, f32[1184,1792]{1,0:T(8,128)} %get-tuple-element.12, f32[1024,1792]{1,0:T(8,128)} %reduce_sum.49, bf16[1024,1792]{1,0:T(8,128)(2,1)} %copy.19), kind=kOutput, calls=%fused_computation.6 | convolution fusion | flops 4359290880 | bytes 30408704 | tf_op jit(solution)/shard_map/dot_general | solution.py:43
  784.5 0.0 collective-permute-done.3
  784.5 69.0 %collective-permute-done.2 = f32[1184,1792]{1,0:T(8,128)} collective-permute-done((f32[1184,1792]{1,0:T(8,128)}, f32[1184,1792]{1,0:T(8,128)}, u32[]{:S(2)}, u32[]{:S(2)}) %collective-permute-start.2) | collective-permute-done | bytes 8486944 | tf_op jit(solution)/shard_map/ppermute | solution.py:9
  853.5 0.0 copy-start.1
  853.5 14.3 %subtract_bitcast_fusion = f32[1,1184,1792]{2,1,0:T(8,128)} fusion(f32[1184,1792]{1,0:T(8,128)S(1)} %fusion.1, f32[1184,1792]{1,0:T(8,128)} %collective-permute-done.3, f32[1184,1792]{1,0:T(8,128)} %collective-permute-done.2, f32[1184,1792]{1,0:T(8,128)} %get-tuple-element.8, f32[]{:T(128)} %get-tuple-element.7, f32[]{:T(128)} %get-tuple-element.6, f32[]{:T(128)S(6)} %sub.29), kind=kLoop, calls=%fused_computation.7 | loop fusion | flops 12730368 | bytes 42434572 | tf_op jit(solution)/shard_map/broadcast_in_dim | solution.py:59
  867.8 0.0 copy-done.1
  (4 shorter events, 0.0 us)
Async XLA Ops:
  6.5 3.3 copy-start
  6.5 58.2 %all-gather.7.cloned.1.call-start = ((), (), s32[]{:S(2)}) async-start(), calls=%async_computation | async-start | bytes 4128768 | tf_op jit(solution)/shard_map/all_gather | solution.py:31
  27.5 73.6 %all-gather.9.cloned.1.call-start = ((), (), s32[]{:S(2)}) async-start(), calls=%async_computation.1 | async-start | bytes 4128768 | tf_op jit(solution)/shard_map/all_gather | solution.py:34
  28.6 341.7 %all-gather.11.cloned.1.call-start = ((), (), s32[]{:S(2)}) async-start(), calls=%async_computation.2 | async-start | bytes 66060288 | tf_op jit(solution)/shard_map/all_gather | solution.py:41
  64.8 7.6 copy-start.3
  64.8 15.6 %slice-start = ((s8[8486912]{0:T(1024)(128)(4,1)}), s8[4194304]{0:T(1024)(128)(4,1)S(1)}, s32[]{:S(2)}) async-start(s8[8486912]{0:T(1024)(128)(4,1)} %bitcast.34), calls=%async_computation.4 | async-start | bytes 8388608
  64.8 15.6 %slice-start.1 = ((s8[8486912]{0:T(1024)(128)(4,1)}), s8[4194304]{0:T(1024)(128)(4,1)S(1)}, s32[]{:S(2)}) async-start(s8[8486912]{0:T(1024)(128)(4,1)} %bitcast.34), calls=%async_computation.5 | async-start | bytes 8388608
  72.4 8.0 slice-start.2
  87.7 3.5 copy-start.2
  87.7 664.3 %all-gather.13.cloned.1.call-start = ((), (), s32[]{:S(2)}) async-start(), calls=%async_computation.3 | async-start | bytes 66060288 | tf_op jit(solution)/shard_map/all_gather | solution.py:41
  87.8 304.5 %collective-permute-start = (f32[1184,1792]{1,0:T(8,128)}, f32[1184,1792]{1,0:T(8,128)}, u32[]{:S(2)}, u32[]{:S(2)}) collective-permute-start(f32[1184,1792]{1,0:T(8,128)} %bitcast.32), channel_id=1, source_target_pairs={{0,24},{8,0},{16,8},{24,16},{1,25},{9,1},{17,9},{25,17},{2,26},{10... | collective-permute-start | bytes 25460744 | tf_op jit(solution)/shard_map/ppermute | solution.py:9
  91.1 365.4 %collective-permute-start.1 = (f32[1184,1792]{1,0:T(8,128)}, f32[1184,1792]{1,0:T(8,128)}, u32[]{:S(2)}, u32[]{:S(2)}) collective-permute-start(f32[1184,1792]{1,0:T(8,128)} %bitcast.33), channel_id=1, source_target_pairs={{0,8},{8,16},{16,24},{24,0},{1,9},{9,17},{17,25},{25,1},{2,10},{10... | collective-permute-start | bytes 25460744 | tf_op jit(solution)/shard_map/ppermute | solution.py:9
  486.2 298.4 %collective-permute-start.3 = (f32[1184,1792]{1,0:T(8,128)}, f32[1184,1792]{1,0:T(8,128)}, u32[]{:S(2)}, u32[]{:S(2)}) collective-permute-start(f32[1184,1792]{1,0:T(8,128)} %get-tuple-element.8), channel_id=1, source_target_pairs={{0,8},{8,16},{16,24},{24,0},{1,9},{9,17},{17,25},{25,1},{2,10},{10... | collective-permute-start | bytes 25460744 | tf_op jit(solution)/shard_map/ppermute | solution.py:9
  487.7 365.8 %collective-permute-start.2 = (f32[1184,1792]{1,0:T(8,128)}, f32[1184,1792]{1,0:T(8,128)}, u32[]{:S(2)}, u32[]{:S(2)}) collective-permute-start(f32[1184,1792]{1,0:T(8,128)} %get-tuple-element.8), channel_id=1, source_target_pairs={{0,24},{8,0},{16,8},{24,16},{1,25},{9,1},{17,9},{25,17},{2,26},{10... | collective-permute-start | bytes 25460744 | tf_op jit(solution)/shard_map/ppermute | solution.py:9
  853.5 14.3 %copy-start.1 = (s32[4,1024]{1,0:T(4,128)S(1)}, s32[4,1024]{1,0:T(4,128)}, u32[]{:S(2)}) copy-start(s32[4,1024]{1,0:T(4,128)} %param.15) | copy-start | bytes 49156
Sparse Core Ops, SparseCore 0:
  27.6 37.0 all-gather.6
  66.7 34.3 all-gather.8
  103.0 267.2 all-gather.10
  486.3 265.6 all-gather.12
